TPU v7x, 128 devices: a whole 4x4x4 slice. The times are simulated.
128 devices in a mesh: depth: 4 (over z), col: 4 (over y), row: 8 (over x, core).
Axes of the slice: x: 4, y: 4, z: 4, core: 2. Of those that a mesh axis runs over, the one named last changes fastest.
Arguments:
- a_mat: bfloat16 [12288, 12288], P('row', 'col')
- b_mat: bfloat16 [12288, 12288], P('row', 'col')
Outputs:
- output: bfloat16 [12288, 12288], P(('row', 'depth'), 'col')
All inputs are finite; a program needn't handle non-finite values.
Results may differ from a plain program's by a relative error of at most 0.001.
Values are sent between devices in bfloat16 or wider.
A program may use at most 1 GiB of HBM per device.

v0:
```python
import jax
import jax.numpy as jnp
from jax import lax
from jax.sharding import PartitionSpec as P

AXES_ALL = ("depth", "col", "row")


def skew_pairs(depth_n, col_n, row_n):
    col_ratio = row_n // col_n
    layer_steps = row_n // depth_n
    pairs_a0 = []
    pairs_a1 = []
    pairs_b = []
    for layer_idx in range(depth_n):
        for col_idx in range(col_n):
            for row_idx in range(row_n):
                target_dev = (layer_idx * col_n + col_idx) * row_n + row_idx
                start_blk = (row_idx + col_ratio * col_idx + layer_idx * layer_steps) % row_n
                coarse_blk = start_blk // col_ratio
                pairs_a0.append(((layer_idx * col_n + coarse_blk) * row_n + row_idx, target_dev))
                pairs_a1.append(((layer_idx * col_n + (coarse_blk + 1) % col_n) * row_n + row_idx, target_dev))
                pairs_b.append(((layer_idx * col_n + col_idx) * row_n + start_blk, target_dev))
    return pairs_a0, pairs_a1, pairs_b


def solution(mesh):
    depth_n = mesh.shape["depth"]
    col_n = mesh.shape["col"]
    row_n = mesh.shape["row"]
    col_ratio = row_n // col_n
    layer_steps = row_n // depth_n
    pairs_a0, pairs_a1, pairs_b = skew_pairs(depth_n, col_n, row_n)
    pairs_col = [((col_idx + 1) % col_n, col_idx) for col_idx in range(col_n)]
    pairs_row = [((row_idx + 1) % row_n, row_idx) for row_idx in range(row_n)]

    def local_mm(a_blk, b_blk):
        layer_idx = lax.axis_index("depth")
        row_idx = lax.axis_index("row")
        fine_side = a_blk.shape[0]
        a_first = lax.ppermute(a_blk, AXES_ALL, pairs_a0)
        if col_ratio > 1:
            a_second = lax.ppermute(a_blk, AXES_ALL, pairs_a1)
            a_joined = jnp.concatenate([a_first, a_second], axis=1)
            offset = ((row_idx + layer_idx * layer_steps) % col_ratio) * fine_side
            a_window = lax.dynamic_slice_in_dim(a_joined, offset, a_blk.shape[1], axis=1)
        else:
            a_window = a_first
        a_parts = [a_window[:, blk_idx * fine_side:(blk_idx + 1) * fine_side] for blk_idx in range(min(col_ratio, layer_steps))]
        b_cur = lax.ppermute(b_blk, AXES_ALL, pairs_b)
        part_sum = None
        for step_idx in range(layer_steps):
            a_cur = a_parts[step_idx]
            block_prod = jnp.dot(a_cur, b_cur, preferred_element_type=jnp.float32)
            part_sum = block_prod if part_sum is None else part_sum + block_prod
            if step_idx + col_ratio < layer_steps:
                a_parts.append(lax.ppermute(a_cur, "col", pairs_col))
            if step_idx + 1 < layer_steps:
                b_cur = lax.ppermute(b_cur, "row", pairs_row)
        c_rows = lax.psum_scatter(part_sum, "depth", scatter_dimension=0, tiled=True)
        return c_rows.astype(jnp.bfloat16)

    spec_in = P("row", "col")
    spec_out = P(("row", "depth"), "col")
    return jax.shard_map(local_mm, mesh=mesh, in_specs=(spec_in, spec_in), out_specs=spec_out, check_vma=False)
```

profile of v0, /device:TPU:32, one launch (start us, length us, event | category | flops | bytes accessed | tf_op | source)
XLA Modules:
  0.0 715.4 jit_solution(7875562438234186641)
XLA Ops:
  6.5 0.0 reduce-scatter.2.cloned.1.call-start
  6.5 4.7 collective-permute-start.2
  11.2 3.8 collective-permute-start.1
  15.0 70.6 %collective-permute-start = (bf16[1536,3072]{1,0:T(8,128)(2,1)}, bf16[1536,3072]{1,0:T(8,128)(2,1)}, u32[]{:S(2)}, u32[]{:S(2)}) collective-permute-start(bf16[1536,3072]{1,0:T(8,128)(2,1)} %param.2), channel_id=1, source_target_pairs={{0,0},{1,1},{10,2},{11,3},{20,4},{21,5},{30,6},{31,7},{8,8},{9,9},... | collective-permute-start | bytes 28311560 | tf_op jit(solution)/shard_map/ppermute | solution.py:41
  85.6 127.7 %collective-permute-done.2 = bf16[1536,3072]{1,0:T(8,128)(2,1)} collective-permute-done((bf16[1536,3072]{1,0:T(8,128)(2,1)}, bf16[1536,3072]{1,0:T(8,128)(2,1)}, u32[]{:S(2)}, u32[]{:S(2)}) %collective-permute-start.2) | collective-permute-done | bytes 9437216 | tf_op jit(solution)/shard_map/ppermute | solution.py:50
  213.3 2.4 collective-permute-start.3
  215.7 3.5 collective-permute-done.1
  219.2 271.0 %collective-permute-done = bf16[1536,3072]{1,0:T(8,128)(2,1)} collective-permute-done((bf16[1536,3072]{1,0:T(8,128)(2,1)}, bf16[1536,3072]{1,0:T(8,128)(2,1)}, u32[]{:S(2)}, u32[]{:S(2)}) %collective-permute-start) | collective-permute-done | bytes 9437216 | tf_op jit(solution)/shard_map/ppermute | solution.py:41
  490.2 6.9 fusion
  497.1 20.0 %fusion.2 = f32[1536,3072]{1,0:T(8,128)} fusion(bf16[1536,3072]{1,0:T(8,128)(2,1)} %collective-permute-done.2, bf16[1536,3072]{1,0:T(8,128)(2,1)S(1)} %fusion), kind=kOutput, calls=%fused_computation.5 | convolution fusion | flops 14495514624 | bytes 33030144 | tf_op jit(solution)/shard_map/dot_general | solution.py:54
  517.0 0.0 collective-permute-done.3
  517.0 22.9 %convolution_add_fusion = f32[1536,3072]{1,0:T(8,128)} fusion(f32[1536,3072]{1,0:T(8,128)} %fusion.2, bf16[1536,3072]{1,0:T(8,128)(2,1)} %collective-permute-done.3, bf16[1536,3072]{1,0:T(8,128)(2,1)S(1)} %fusion), kind=kOutput, calls=%fused_computation.2 | convolution fusion | flops 14500233216 | bytes 51904512 | tf_op jit(solution)/shard_map/dot_general | solution.py:54
  539.9 0.0 reduce-scatter.2.cloned.1.call-update
  540.0 164.5 %reduce-scatter.2.cloned.1.call-done = f32[384,3072]{1,0:T(8,128)} async-done(((f32[1536,3072]{1,0:T(8,128)}), f32[384,3072]{1,0:T(8,128)}) %reduce-scatter.2.cloned.1.call-update) | async-done | bytes 4718608 | tf_op jit(solution)/shard_map/reduce_scatter | solution.py:60
  704.5 4.1 convert_element_type.3
Async XLA Ops:
  6.5 697.9 %reduce-scatter.2.cloned.1.call-start = ((), (), s32[]{:S(2)}) async-start(), calls=%async_computation.1 | async-start | bytes 23592960 | tf_op jit(solution)/shard_map/reduce_scatter | solution.py:60
  6.5 206.8 %collective-permute-start.2 = (bf16[1536,3072]{1,0:T(8,128)(2,1)}, bf16[1536,3072]{1,0:T(8,128)(2,1)}, u32[]{:S(2)}, u32[]{:S(2)}) collective-permute-start(bf16[1536,3072]{1,0:T(8,128)(2,1)} %param.3), channel_id=1, source_target_pairs={{0,0},{1,1},{2,2},{3,3},{4,4},{5,5},{6,6},{7,7},{10,8},{11,9},{12,... | collective-permute-start | bytes 28311560 | tf_op jit(solution)/shard_map/ppermute | solution.py:50
  11.2 208.0 %collective-permute-start.1 = (bf16[1536,3072]{1,0:T(8,128)(2,1)}, bf16[1536,3072]{1,0:T(8,128)(2,1)}, u32[]{:S(2)}, u32[]{:S(2)}) collective-permute-start(bf16[1536,3072]{1,0:T(8,128)(2,1)} %param.2), channel_id=1, source_target_pairs={{8,0},{9,1},{18,2},{19,3},{28,4},{29,5},{6,6},{7,7},{16,8},{17,9},... | collective-permute-start | bytes 28311560 | tf_op jit(solution)/shard_map/ppermute | solution.py:43
  15.0 475.1 %collective-permute-start = (bf16[1536,3072]{1,0:T(8,128)(2,1)}, bf16[1536,3072]{1,0:T(8,128)(2,1)}, u32[]{:S(2)}, u32[]{:S(2)}) collective-permute-start(bf16[1536,3072]{1,0:T(8,128)(2,1)} %param.2), channel_id=1, source_target_pairs={{0,0},{1,1},{10,2},{11,3},{20,4},{21,5},{30,6},{31,7},{8,8},{9,9},... | collective-permute-start | bytes 28311560 | tf_op jit(solution)/shard_map/ppermute | solution.py:41
  213.3 303.7 %collective-permute-start.3 = (bf16[1536,3072]{1,0:T(8,128)(2,1)}, bf16[1536,3072]{1,0:T(8,128)(2,1)}, u32[]{:S(2)}, u32[]{:S(2)}) collective-permute-start(bf16[1536,3072]{1,0:T(8,128)(2,1)} %collective-permute-done.2), channel_id=1, source_target_pairs={{1,0},{2,1},{3,2},{4,3},{5,4},{6,5},{7,6},{0,7},{9,8},{10,9},{11,1... | collective-permute-start | bytes 28311560 | tf_op jit(solution)/shard_map/ppermute | solution.py:59
Sparse Core Ops, SparseCore 0:
  540.1 164.3 reduce-scatter.1
where the time goes:
time: 728 us; the launch traced here: 715 us
  waiting for transfers between devices  567 us (78%)
  starting transfers between devices  81.5 us (11%)
  matrix products  42.9 us (6%)
  between operations  13.4 us (2%)
  other arithmetic  11 us (2%)
    ppermute x1, waiting for transfers between devices, local_mm(): a_first = lax.ppermute(a_blk, AXES_ALL, pairs_a0)  271 us
    reduce_scatter x1, waiting for transfers between devices, local_mm(): lax.psum_scatter(part_sum, 'depth', scatter_dimension=0, tiled=True)  165 us
    ppermute x1, waiting for transfers between devices, local_mm(): b_cur = lax.ppermute(b_blk, AXES_ALL, pairs_b)  128 us
    ppermute x1, starting transfers between devices, local_mm(): a_first = lax.ppermute(a_blk, AXES_ALL, pairs_a0)  70.6 us
    dot_general x2, matrix products, local_mm(): block_prod = jnp.dot(a_cur, b_cur, preferred_element_type=jnp.float32)  42.9 us
  transfers between devices with their start and end apart: 5, of which 4 were waited for; matrix products, arithmetic and copies ran while one was open for 4% of the time, Pallas kernels for 0%

commit v1 on v0

v1 whole, which is shorter than its diff:
```python
import functools

import jax
import jax.numpy as jnp
from jax import lax
from jax.experimental import pallas as pl
from jax.experimental.pallas import tpu as pltpu
from jax.sharding import PartitionSpec as P

MESH = pl.DeviceIdType.MESH

A_OWN, A_FWD, A_Z = 0, 4, 6
B_OWN, B_FWD, B_Z, B_D2D = 9, 11, 13, 16
KINDS = 20
LAG = 4


def kernel(steps, seg, a_ref, b_ref, c_ref, a_buf, b_buf, acc, c_st, snd, rcv, loc, c_snd, c_rcv, c_loc):
    band, kblk = a_ref.shape
    half_m, half_n = band // 2, kblk // 2
    third_m, third_n = half_m // 3, half_n // 3
    l = lax.axis_index("depth")
    y = lax.axis_index("col")
    i = lax.axis_index("row")
    x, c = i // 2, lax.rem(i, 2)
    h, e = l // 2, lax.rem(l, 2)
    n = lax.rem((l + 1) // 2, 2)
    role_a, role_b = e, h
    yp, ym, y2 = lax.rem(y + 1, 4), lax.rem(y + 3, 4), lax.rem(y + 2, 4)
    xp, xm, x2 = lax.rem(x + 1, 4), lax.rem(x + 3, 4), lax.rem(x + 2, 4)
    dev_yp, dev_ym = {"col": yp}, {"col": ym}
    dev_xp, dev_xm = {"row": 2 * xp + c}, {"row": 2 * xm + c}
    dev_za, dev_zb = {"depth": l + 1 - 2 * e}, {"depth": 3 - l}
    dev_sib = {"row": i + 1 - 2 * c}

    def al(v, m=128):
        return pl.multiple_of(v, m)

    def remote(kind, q, src, dst, dev):
        return pltpu.make_async_remote_copy(
            src_ref=src, dst_ref=dst, send_sem=snd.at[kind, q], recv_sem=rcv.at[kind, q], device_id=dev, device_id_type=MESH
        )

    def a_own(q):
        out = []
        for d, dev in enumerate((dev_yp, dev_ym)):
            for p in range(2):
                src = a_ref.at[pl.ds(al(h * half_m + third_m * role_a), 2 * third_m), pl.ds(al(p * band + q * seg), seg)]
                dst = a_buf.at[q, pl.ds(al(third_m * role_a), 2 * third_m), pl.ds(al((2 * y + p) * seg), seg)]
                out.append(remote(A_OWN + 2 * d + p, q, src, dst, dev))
        return out

    def a_fwd(q):
        out = []
        for d, (blk, dev) in enumerate(((ym, dev_yp), (yp, dev_ym))):
            ref = a_buf.at[q, pl.ds(al(third_m * (role_a + d)), third_m), pl.ds(al(2 * blk * seg), 2 * seg)]
            out.append(remote(A_FWD + d, q, ref, ref, dev))
        return out

    def a_z(q, which):
        blk = (ym, yp, y2)[which]
        ref = a_buf.at[q, pl.ds(al(2 * third_m * role_a), third_m), pl.ds(al(2 * blk * seg), 2 * seg)]
        return remote(A_Z + which, q, ref, ref, dev_za)

    def b_own(q):
        out = []
        for d, dev in enumerate((dev_xp, dev_xm)):
            src = b_ref.at[pl.ds(al(q * seg), seg), pl.ds(al(n * half_n + third_n * role_b), 2 * third_n)]
            dst = b_buf.at[q, pl.ds(al((2 * x + c) * seg), seg), pl.ds(al(third_n * role_b), 2 * third_n)]
            out.append(remote(B_OWN + d, q, src, dst, dev))
        return out

    def b_fwd(q):
        out = []
        for d, (blk, dev) in enumerate(((xm, dev_xp), (xp, dev_xm))):
            ref = b_buf.at[q, pl.ds(al((2 * blk + c) * seg), seg), pl.ds(al(third_n * (role_b + d)), third_n)]
            out.append(remote(B_FWD + d, q, ref, ref, dev))
        return out

    def b_z(q, which):
        blk = (xm, xp, x2)[which]
        ref = b_buf.at[q, pl.ds(al((2 * blk + c) * seg), seg), pl.ds(al(2 * third_n * role_b), third_n)]
        return remote(B_Z + which, q, ref, ref, dev_zb)

    def b_d2d(q, which):
        blk = (xm, xp, x2, x)[which]
        dst = b_buf.at[q, pl.ds(al((2 * blk + c) * seg), seg), :]
        src = b_ref.at[pl.ds(al(q * seg), seg), pl.ds(al(n * half_n), half_n)] if which == 3 else dst
        return remote(B_D2D + which, q, src, dst, dev_sib)

    def local(q):
        out = []
        for p in range(2):
            src = a_ref.at[pl.ds(al(h * half_m), half_m), pl.ds(al(p * band + q * seg), seg)]
            dst = a_buf.at[q, :, pl.ds(al((2 * y + p) * seg), seg)]
            out.append(pltpu.make_async_copy(src, dst, loc.at[p, q]))
        src = b_ref.at[pl.ds(al(q * seg), seg), pl.ds(al(n * half_n), half_n)]
        dst = b_buf.at[q, pl.ds(al((2 * x + c) * seg), seg), :]
        out.append(pltpu.make_async_copy(src, dst, loc.at[2, q]))
        return out

    barrier = pltpu.get_barrier_semaphore()
    partners = (dev_yp, dev_ym, dev_xp, dev_xm, dev_za, dev_zb, dev_sib)
    for dev in partners:
        pl.semaphore_signal(barrier, inc=1, device_id=dev, device_id_type=MESH)
    pl.semaphore_wait(barrier, len(partners))

    tile_n = third_n

    def zero_tile(r, _):
        acc[pl.ds(al(r * 64, 64), 64), :] = jnp.zeros((64, half_n), jnp.float32)
        return 0

    def wait_inputs(q):
        for cp in local(q):
            cp.wait()
        for which in range(3):
            a_z(q, which).wait_recv()
        for which in range(4):
            b_d2d(q, which).wait_recv()

    def send_own(q):
        for cp in b_own(q) + a_own(q) + [b_d2d(q, 3)] + local(q):
            cp.start()

    def first_hop(q):
        for cp in b_own(q):
            cp.wait_recv()
        for cp in b_fwd(q) + [b_z(q, 0), b_z(q, 1)]:
            cp.start()
        for cp in a_own(q):
            cp.wait_recv()
        for cp in a_fwd(q) + [a_z(q, 0), a_z(q, 1)]:
            cp.start()

    def second_hop(q):
        for cp in b_fwd(q):
            cp.wait_recv()
        b_z(q, 2).start()
        for cp in a_fwd(q):
            cp.wait_recv()
        a_z(q, 2).start()
        for which in range(2):
            b_z(q, which).wait_recv()
            b_d2d(q, which).start()

    def last_hop(q):
        b_z(q, 2).wait_recv()
        b_d2d(q, 2).start()

    def compute(q):
        wait_inputs(q)

        def tile(j, _):
            rows = pl.ds(al((j // 3) * third_m), third_m)
            cols = pl.ds(al(lax.rem(j, 3) * tile_n), tile_n)
            acc[rows, cols] += jnp.dot(a_buf[q, rows, :], b_buf[q, :, cols], preferred_element_type=jnp.float32)
            return 0

        lax.fori_loop(0, 9, tile, 0)

    def body(t, _):
        pl.when(t < steps)(lambda: send_own(t))

        @pl.when(t == 0)
        def _():
            lax.fori_loop(0, half_m // 64, zero_tile, 0)

        pl.when(jnp.logical_and(t >= 1, t < steps + 1))(lambda: first_hop(t - 1))
        pl.when(jnp.logical_and(t >= 2, t < steps + 2))(lambda: second_hop(t - 2))
        pl.when(jnp.logical_and(t >= 3, t < steps + 3))(lambda: last_hop(t - 3))
        pl.when(jnp.logical_and(t >= LAG, t < steps + LAG - 1))(lambda: compute(t - LAG))
        return 0

    lax.fori_loop(0, steps + LAG, body, 0)

    q_last = steps - 1
    wait_inputs(q_last)
    quarter = half_m // 2
    chunk = quarter // 3

    def finish(row0):
        def tile(j, _):
            rows = pl.ds(al(row0), chunk)
            cols = pl.ds(al(j * tile_n), tile_n)
            total = acc[rows, cols] + jnp.dot(
                a_buf[q_last, rows, :], b_buf[q_last, :, cols], preferred_element_type=jnp.float32
            )
            c_st[rows, cols] = total.astype(c_st.dtype)
            return 0

        lax.fori_loop(0, 3, tile, 0)

    col_out = pl.ds(al(n * half_n), half_n)

    def c_remote(k):
        row0 = al((1 - e) * quarter + k * chunk)
        return pltpu.make_async_remote_copy(
            src_ref=c_st.at[pl.ds(row0, chunk), :],
            dst_ref=c_ref.at[pl.ds(al(k * chunk), chunk), col_out],
            send_sem=c_snd.at[k],
            recv_sem=c_rcv.at[k],
            device_id=dev_za,
            device_id_type=MESH,
        )

    def c_local(k):
        row0 = al(e * quarter + k * chunk)
        return pltpu.make_async_copy(c_st.at[pl.ds(row0, chunk), :], c_ref.at[pl.ds(al(k * chunk), chunk), col_out], c_loc.at[k])

    def out_partner(k, _):
        finish((1 - e) * quarter + k * chunk)
        c_remote(k).start()
        return 0

    def out_own(k, _):
        finish(e * quarter + k * chunk)
        c_local(k).start()
        return 0

    lax.fori_loop(0, 3, out_partner, 0)
    lax.fori_loop(0, 3, out_own, 0)

    def drain(q, _):
        for cp in a_own(q) + a_fwd(q) + b_own(q) + b_fwd(q):
            cp.wait_send()
        for which in range(3):
            a_z(q, which).wait_send()
            b_z(q, which).wait_send()
        for which in range(4):
            b_d2d(q, which).wait_send()
        return 0

    lax.fori_loop(0, steps, drain, 0)

    def drain_c(k, _):
        c_local(k).wait()
        c_remote(k).wait()
        return 0

    lax.fori_loop(0, 3, drain_c, 0)


def solution(mesh):
    assert (mesh.shape["depth"], mesh.shape["col"], mesh.shape["row"]) == (4, 4, 8)

    def local_mm(a_blk, b_blk):
        band, kblk = a_blk.shape
        seg = 128
        steps = band // seg
        half_m, half_n = band // 2, kblk // 2
        return pl.pallas_call(
            functools.partial(kernel, steps, seg),
            out_shape=jax.ShapeDtypeStruct((band // 4, kblk), jnp.bfloat16),
            in_specs=[pl.BlockSpec(memory_space=pl.ANY)] * 2,
            out_specs=pl.BlockSpec(memory_space=pl.ANY),
            scratch_shapes=[
                pltpu.VMEM((steps, half_m, 8 * seg), jnp.bfloat16),
                pltpu.VMEM((steps, 8 * seg, half_n), jnp.bfloat16),
                pltpu.VMEM((half_m, half_n), jnp.float32),
                pltpu.VMEM((half_m, half_n), jnp.bfloat16),
                pltpu.SemaphoreType.DMA((KINDS, steps)),
                pltpu.SemaphoreType.DMA((KINDS, steps)),
                pltpu.SemaphoreType.DMA((3, steps)),
                pltpu.SemaphoreType.DMA((3,)),
                pltpu.SemaphoreType.DMA((3,)),
                pltpu.SemaphoreType.DMA((3,)),
            ],
            compiler_params=pltpu.CompilerParams(collective_id=0, has_side_effects=True, vmem_limit_bytes=67043328),
            cost_estimate=pl.CostEstimate(
                flops=2 * half_m * half_n * 8 * band, bytes_accessed=4 * band * kblk, transcendentals=0
            ),
            name="gather_mm",
        )(a_blk, b_blk)

    spec_in = P("row", "col")
    spec_out = P(("row", "depth"), "col")
    return jax.shard_map(local_mm, mesh=mesh, in_specs=(spec_in, spec_in), out_specs=spec_out, check_vma=False)
```

time: 728 us -> 156 us (0.21); the launches traced: 715 us -> 156 us
  waiting for transfers between devices: 567 us -> 0 us
  Pallas kernels: 0 us -> 153 us
  starting transfers between devices: 81.5 us -> 0 us
  matrix products: 42.9 us -> 0 us
  between operations: 13.4 us -> 0.01 us
  other arithmetic: 11 us -> 0 us
    ppermute x4 -> x0, waiting for transfers between devices: 402 us -> none  [the longest x1 271 us: local_mm(): a_first = lax.ppermute(a_blk, AXES_ALL, pairs_a0)]
    reduce_scatter x1 -> x0, waiting for transfers between devices: 165 us -> none  [local_mm(): lax.psum_scatter(part_sum, 'depth', scatter_dimension=0, tiled=True)]
    pallas_call x0 -> x1, Pallas kernels: none -> 153 us  [local_mm(): pl.pallas_call(functools.partial(kernel, steps, seg), out_shape=jax.Shape...]
    ppermute x4 -> x0, starting transfers between devices: 81.5 us -> none  [the longest x1 70.6 us: local_mm(): a_first = lax.ppermute(a_blk, AXES_ALL, pairs_a0)]
    dot_general x2 -> x0, matrix products: 42.9 us -> none  [local_mm(): block_prod = jnp.dot(a_cur, b_cur, preferred_element_type=jnp.float32)]
  transfers between devices with their start and end apart: 5 -> 0, of which waited for: 4 -> 0; matrix products, arithmetic and copies ran while one was open for 4% -> 0% of each run, Pallas kernels for 0% -> 0%
where the time goes in v1:
time: 156 us
  Pallas kernels  153 us (98%)
  local copies, waits for them, and re-layouts  3.22 us (2%)
    pallas_call x1, Pallas kernels, local_mm(): pl.pallas_call(functools.partial(kernel, steps, seg), out_shape=jax.Shape...  153 us
    unnamed x1, local copies, waits for them, and re-layouts  3.22 us

profile of v1, /device:TPU:32, one launch (start us, length us, event | category | flops | bytes accessed | tf_op | source)
XLA Modules:
  0.0 156.3 jit_solution(6548902217449545564)
XLA Ops:
  0.0 153.1 %gather_mm.1 = bf16[384,3072]{1,0:T(8,128)(2,1)} custom-call(bf16[1536,3072]{1,0:T(8,128)(2,1)} %a_ref.1, bf16[1536,3072]{1,0:T(8,128)(2,1)} %b_ref.1), custom_call_target="tpu_custom_call" | custom-call | flops 28991029248 | bytes 18874368 | tf_op jit(solution)/shard_map/gather_mm/pallas_call | solution.py:252
  153.1 3.2 %copy.4 = bf16[384,3072]{1,0:T(8,128)(2,1)} copy(bf16[384,3072]{1,0:T(8,128)(2,1)} %gather_mm.1) | data formatting | bytes 4718592

commit v2 on v0

v2 whole, which is shorter than its diff:
```python
import functools

import jax
import jax.numpy as jnp
from jax import lax
from jax.experimental import pallas as pl
from jax.experimental.pallas import tpu as pltpu
from jax.sharding import PartitionSpec as P

MESH = pl.DeviceIdType.MESH

A_OWN, A_FWD, A_Z, B_OWN, B_FWD, B_Z, B_D2D, B_Z2, A_LOC, B_LOC = range(10)
KINDS = 10
SLOTS = 8

PHASES = ((192, 64, 768), (128, 32, 512), (64, 16, 256))
SEG = 256
EXCL_B = 80
AHEAD, HOP1, HOP2, HOP3, LAG = 0, 1, 2, 3, 4


def kernel(steps, a_ref, b_ref, c_ref, a_buf, b_buf, acc, c_st, snd, rcv, c_snd, c_rcv, c_loc):
    _, sub, kblk = a_ref.shape
    band, half_n = b_ref.shape[0], kblk // 2
    l = lax.axis_index("depth")
    y = lax.axis_index("col")
    i = lax.axis_index("row")
    x, c = i // 2, lax.rem(i, 2)
    h, e = l // 2, lax.rem(l, 2)
    n = lax.rem((l + 1) // 2, 2)
    role_a, role_b = e, h
    yp, ym, y2 = lax.rem(y + 1, 4), lax.rem(y + 3, 4), lax.rem(y + 2, 4)
    xp, xm, x2 = lax.rem(x + 1, 4), lax.rem(x + 3, 4), lax.rem(x + 2, 4)
    dev_yp, dev_ym = {"col": yp}, {"col": ym}
    dev_xp, dev_xm = {"row": 2 * xp + c}, {"row": 2 * xm + c}
    dev_za, dev_zb = {"depth": l + 1 - 2 * e}, {"depth": 3 - l}
    dev_sib = {"row": i + 1 - 2 * c}
    starts, r_at, c_at = [], 0, 0
    for rows, _, cols in PHASES:
        starts.append((r_at, c_at))
        r_at, c_at = r_at + rows, c_at + cols

    def al(v, m=128):
        return pl.multiple_of(v, m)

    def slot(ph, q):
        return lax.rem(ph * steps + q, SLOTS)

    def remote(kind, ph, q, src, dst, dev):
        return pltpu.make_async_remote_copy(
            src_ref=src,
            dst_ref=dst,
            send_sem=snd.at[B_Z if kind == B_Z2 else kind],
            recv_sem=rcv.at[kind, slot(ph, q)],
            device_id=dev,
            device_id_type=MESH,
        )

    def arrived(kind, ph, q):
        r0, (rows, excl, _) = starts[ph][0], PHASES[ph]
        if kind in (A_OWN, A_FWD, A_Z, A_LOC):
            count, width = {A_OWN: (rows - excl, 4), A_FWD: (rows - excl, 2), A_Z: (excl, 6), A_LOC: (rows, 2)}[kind]
            ref = a_buf.at[q, :, pl.ds(0, count), pl.ds(0, width * SEG)]
        else:
            carry = SEG - EXCL_B
            count = {B_OWN: 2 * carry, B_FWD: carry, B_Z: 2 * EXCL_B, B_Z2: EXCL_B, B_D2D: 4 * SEG, B_LOC: SEG}[kind]
            ref = b_buf.at[q, pl.ds(0, count), cols_b(ph)]
        pltpu.make_async_copy(ref, ref, rcv.at[kind, slot(ph, q)]).wait()

    def lanes_a(blk, p=0, width=2 * SEG):
        return pl.ds(al((2 * blk + p) * SEG), width)

    def a_own(ph, q):
        rows, excl, _ = PHASES[ph]
        carry = pl.ds(al(starts[ph][0] + excl * role_a, 16), rows - excl)
        out = []
        for d, dev in enumerate((dev_yp, dev_ym)):
            for p in range(2):
                src = a_ref.at[pl.ds(2 * h, 2), carry, pl.ds(al(p * band + q * SEG), SEG)]
                dst = a_buf.at[q, :, carry, lanes_a(y, p, SEG)]
                out.append(remote(A_OWN, ph, q, src, dst, dev))
        return out

    def a_fwd(ph, q):
        rows, excl, _ = PHASES[ph]
        carry = pl.ds(al(starts[ph][0] + excl * role_a, 16), rows - excl)
        out = []
        for d, (blk, dev) in enumerate(((ym, dev_yp), (yp, dev_ym))):
            ref = a_buf.at[q, :, carry, lanes_a(blk, d, SEG)]
            out.append(remote(A_FWD, ph, q, ref, ref, dev))
        return out

    def a_z(ph, q, which):
        rows, excl, _ = PHASES[ph]
        only = pl.ds(al(starts[ph][0] + (rows - excl) * role_a, 16), excl)
        ref = a_buf.at[q, :, only, lanes_a((ym, yp, y2)[which])]
        return remote(A_Z, ph, q, ref, ref, dev_za)

    def cols_b(ph, base=0):
        return pl.ds(al(base + starts[ph][1]), PHASES[ph][2])

    def b_own(ph, q):
        out = []
        for d, dev in enumerate((dev_xp, dev_xm)):
            src = b_ref.at[pl.ds(al(q * SEG + EXCL_B * role_b, 16), SEG - EXCL_B), cols_b(ph, n * half_n)]
            dst = b_buf.at[q, pl.ds(al((2 * x + c) * SEG + EXCL_B * role_b, 16), SEG - EXCL_B), cols_b(ph)]
            out.append(remote(B_OWN, ph, q, src, dst, dev))
        return out

    def b_fwd(ph, q):
        half = PHASES[ph][2] // 2
        out = []
        for d, (blk, dev) in enumerate(((xm, dev_xp), (xp, dev_xm))):
            ref = b_buf.at[
                q,
                pl.ds(al((2 * blk + c) * SEG + EXCL_B * role_b, 16), SEG - EXCL_B),
                pl.ds(starts[ph][1] + d * half, half),
            ]
            out.append(remote(B_FWD, ph, q, ref, ref, dev))
        return out

    def b_z(ph, q, which):
        blk = (xm, xp, x2)[which]
        ref = b_buf.at[q, pl.ds(al((2 * blk + c) * SEG + (SEG - EXCL_B) * role_b, 16), EXCL_B), cols_b(ph)]
        return remote(B_Z2 if which == 2 else B_Z, ph, q, ref, ref, dev_zb)

    def b_d2d(ph, q, which):
        blk = (xm, xp, x2, x)[which]
        dst = b_buf.at[q, pl.ds(al((2 * blk + c) * SEG), SEG), cols_b(ph)]
        src = b_ref.at[pl.ds(al(q * SEG), SEG), cols_b(ph, n * half_n)] if which == 3 else dst
        return remote(B_D2D, ph, q, src, dst, dev_sib)

    def local(ph, q):
        rows = pl.ds(starts[ph][0], PHASES[ph][0])
        out = []
        for p in range(2):
            src = a_ref.at[pl.ds(2 * h, 2), rows, pl.ds(al(p * band + q * SEG), SEG)]
            dst = a_buf.at[q, :, rows, lanes_a(y, p, SEG)]
            out.append(pltpu.make_async_copy(src, dst, rcv.at[A_LOC, slot(ph, q)]))
        src = b_ref.at[pl.ds(al(q * SEG), SEG), cols_b(ph, n * half_n)]
        dst = b_buf.at[q, pl.ds(al((2 * x + c) * SEG), SEG), cols_b(ph)]
        out.append(pltpu.make_async_copy(src, dst, rcv.at[B_LOC, slot(ph, q)]))
        return out

    barrier = pltpu.get_barrier_semaphore()
    partners = (dev_yp, dev_ym, dev_xp, dev_xm, dev_za, dev_zb, dev_sib)
    for dev in partners:
        pl.semaphore_signal(barrier, inc=1, device_id=dev, device_id_type=MESH)
    pl.semaphore_wait(barrier, len(partners))

    def send_own(ph, q):
        for cp in b_own(ph, q) + a_own(ph, q) + [b_d2d(ph, q, 3)] + local(ph, q):
            cp.start()

    def first_hop(ph, q):
        arrived(B_OWN, ph, q)
        for cp in b_fwd(ph, q) + [b_z(ph, q, 0), b_z(ph, q, 1)]:
            cp.start()
        arrived(A_OWN, ph, q)
        for cp in a_fwd(ph, q) + [a_z(ph, q, 0), a_z(ph, q, 1)]:
            cp.start()

    def second_hop(ph, q):
        arrived(B_FWD, ph, q)
        b_z(ph, q, 2).start()
        arrived(A_FWD, ph, q)
        a_z(ph, q, 2).start()
        arrived(B_Z, ph, q)
        for which in range(2):
            b_d2d(ph, q, which).start()

    def last_hop(ph, q):
        arrived(B_Z2, ph, q)
        b_d2d(ph, q, 2).start()

    def mm(q, r0, rows, col, width):
        a_val = a_buf[q, :, r0 : r0 + rows, :].reshape(2 * rows, 8 * SEG)
        prod = jnp.dot(a_val, b_buf[q, :, pl.ds(col, width)], preferred_element_type=jnp.float32)
        at = (slice(None), slice(r0, r0 + rows), pl.ds(col, width))
        old = jnp.where(q == 0, 0.0, acc[at])
        acc[at] = old + prod.reshape(2, rows, width)

    def strips(ph):
        (r0, c0), (rows, _, cols) = starts[ph], PHASES[ph]
        return ([(0, r0, c0, cols)] if r0 else []) + [(r0, rows, 0, c0 + cols)]

    col_base = n * half_n

    def c_copy(ph, k):
        r0, rows, c0, cols = strips(ph)[k]
        dst = c_ref.at[pl.ds(r0, rows), pl.ds(al(col_base + c0), cols)]
        part = (pl.ds(r0, rows), pl.ds(c0, cols))
        idx = 2 * ph + k
        out = pltpu.make_async_remote_copy(
            src_ref=c_st.at[(1 - e, *part)],
            dst_ref=dst,
            send_sem=c_snd.at[idx],
            recv_sem=c_rcv.at[idx],
            device_id=dev_za,
            device_id_type=MESH,
        )
        return out, pltpu.make_async_copy(c_st.at[(e, *part)], dst, c_loc.at[idx])

    def compute(ph, q):
        for kind in (A_LOC, B_LOC, A_Z, B_D2D):
            arrived(kind, ph, q)
        for k, (r0, rows, c0, cols) in enumerate(strips(ph)):
            mm(q, r0, rows, c0, cols)

            @pl.when(q == steps - 1)
            def _(k=k, r0=r0, rows=rows, c0=c0, cols=cols):
                tile = 256

                def round_tile(j, _, tile=tile):
                    at = (slice(None), slice(r0, r0 + rows), pl.ds(al(c0 + j * tile), tile))
                    c_st[at] = acc[at].astype(c_st.dtype)
                    return 0

                lax.fori_loop(0, cols // tile, round_tile, 0)
                for cp in c_copy(ph, k):
                    cp.start()

    total = len(PHASES) * steps

    def stage(t, delay, fn):
        for ph in range(len(PHASES)):
            q = t - delay - ph * steps
            pl.when(jnp.logical_and(q >= 0, q < steps))(lambda ph=ph, q=q: fn(ph, q))

    for s in range(AHEAD):
        send_own(s // steps, s % steps)

    def body(t, _):
        stage(t, -AHEAD, send_own)
        stage(t, HOP1, first_hop)
        stage(t, HOP2, second_hop)
        stage(t, HOP3, last_hop)
        stage(t, LAG, compute)
        return 0

    lax.fori_loop(0, total + LAG, body, 0)

    carry_a, excl_a = sum(p[0] - p[1] for p in PHASES), sum(p[1] for p in PHASES)
    sent_a = {A_OWN: (carry_a, 4), A_FWD: (carry_a, 2), A_Z: (excl_a, 6)}
    sent_b = {B_OWN: 2 * (SEG - EXCL_B), B_FWD: SEG - EXCL_B, B_Z: 3 * EXCL_B, B_D2D: 4 * SEG}
    for kind, (count, width) in sent_a.items():
        ref = a_buf.at[:, :, pl.ds(0, count), pl.ds(0, width * SEG)]
        pltpu.make_async_copy(ref, ref, snd.at[kind]).wait()
    for kind, count in sent_b.items():
        ref = b_buf.at[:, pl.ds(0, count), :]
        pltpu.make_async_copy(ref, ref, snd.at[kind]).wait()
    for ph in range(len(PHASES)):
        for k in range(len(strips(ph))):
            for cp in c_copy(ph, k):
                cp.wait()


def solution(mesh):
    assert (mesh.shape["depth"], mesh.shape["col"], mesh.shape["row"]) == (4, 4, 8)

    def local_mm(a_blk, b_blk):
        band, kblk = a_blk.shape
        sub, half_n, steps = band // 4, kblk // 2, band // SEG
        assert sum(p[0] for p in PHASES) == sub and sum(p[2] for p in PHASES) == half_n
        return pl.pallas_call(
            functools.partial(kernel, steps),
            out_shape=jax.ShapeDtypeStruct((sub, kblk), jnp.bfloat16),
            in_specs=[pl.BlockSpec(memory_space=pl.ANY)] * 2,
            out_specs=pl.BlockSpec(memory_space=pl.ANY),
            scratch_shapes=[
                pltpu.VMEM((steps, 2, sub, 8 * SEG), jnp.bfloat16),
                pltpu.VMEM((steps, 8 * SEG, half_n), jnp.bfloat16),
                pltpu.VMEM((2, sub, half_n), jnp.float32),
                pltpu.VMEM((2, sub, half_n), jnp.bfloat16),
                pltpu.SemaphoreType.DMA((B_Z2,)),
                pltpu.SemaphoreType.DMA((KINDS, SLOTS)),
                pltpu.SemaphoreType.DMA((2 * len(PHASES),)),
                pltpu.SemaphoreType.DMA((2 * len(PHASES),)),
                pltpu.SemaphoreType.DMA((2 * len(PHASES),)),
            ],
            compiler_params=pltpu.CompilerParams(collective_id=0, has_side_effects=True, vmem_limit_bytes=67043328),
            cost_estimate=pl.CostEstimate(
                flops=4 * sub * half_n * 8 * band, bytes_accessed=4 * band * kblk, transcendentals=0
            ),
            name="gather_mm",
        )(a_blk.reshape(4, sub, kblk), b_blk)

    spec_in = P("row", "col")
    spec_out = P(("row", "depth"), "col")
    return jax.shard_map(local_mm, mesh=mesh, in_specs=(spec_in, spec_in), out_specs=spec_out, check_vma=False)
```

time: 728 us -> 149 us (0.20); the launches traced: 715 us -> 147 us
  waiting for transfers between devices: 567 us -> 0 us
  Pallas kernels: 0 us -> 143 us
  starting transfers between devices: 81.5 us -> 0 us
  matrix products: 42.9 us -> 0 us
  between operations: 13.4 us -> 0.01 us
  other arithmetic: 11 us -> 0 us
    ppermute x4 -> x0, waiting for transfers between devices: 402 us -> none  [the longest x1 271 us: local_mm(): a_first = lax.ppermute(a_blk, AXES_ALL, pairs_a0)]
    reduce_scatter x1 -> x0, waiting for transfers between devices: 165 us -> none  [local_mm(): lax.psum_scatter(part_sum, 'depth', scatter_dimension=0, tiled=True)]
    pallas_call x0 -> x1, Pallas kernels: none -> 143 us  [local_mm(): pl.pallas_call(functools.partial(kernel, steps), out_shape=jax.ShapeDtype...]
    ppermute x4 -> x0, starting transfers between devices: 81.5 us -> none  [the longest x1 70.6 us: local_mm(): a_first = lax.ppermute(a_blk, AXES_ALL, pairs_a0)]
    dot_general x2 -> x0, matrix products: 42.9 us -> none  [local_mm(): block_prod = jnp.dot(a_cur, b_cur, preferred_element_type=jnp.float32)]
  transfers between devices with their start and end apart: 5 -> 0, of which waited for: 4 -> 0; matrix products, arithmetic and copies ran while one was open for 4% -> 0% of each run, Pallas kernels for 0% -> 0%
where the time goes in v2:
time: 149 us; the launch traced here: 147 us
  Pallas kernels  143 us (96%)
  local copies, waits for them, and re-layouts  3.22 us (2%)
    pallas_call x1, Pallas kernels, local_mm(): pl.pallas_call(functools.partial(kernel, steps), out_shape=jax.ShapeDtype...  143 us
    unnamed x1, local copies, waits for them, and re-layouts  3.22 us

profile of v2, /device:TPU:32, one launch (start us, length us, event | category | flops | bytes accessed | tf_op | source)
XLA Modules:
  0.0 146.7 jit_solution(9089299798759826750)
XLA Ops:
  0.0 143.4 %gather_mm.1 = bf16[384,3072]{1,0:T(8,128)(2,1)} custom-call(bf16[4,384,3072]{2,1,0:T(8,128)(2,1)} %bitcast.1, bf16[1536,3072]{1,0:T(8,128)(2,1)} %b_ref.1), custom_call_target="tpu_custom_call" | custom-call | flops 28991029248 | bytes 18874368 | tf_op jit(solution)/shard_map/gather_mm/pallas_call | solution.py:265
  143.4 3.2 %copy.4 = bf16[384,3072]{1,0:T(8,128)(2,1)} copy(bf16[384,3072]{1,0:T(8,128)(2,1)} %gather_mm.1) | data formatting | bytes 4718592

commit v3 on v2

--- a/solution.py
+++ b/solution.py
@@ -14,9 +14,11 @@
 SLOTS = 8
 
 PHASES = ((192, 64, 768), (128, 32, 512), (64, 16, 256))
+WIDTHS = ((768,), (512, 640), (256, 768))
 SEG = 256
 EXCL_B = 80
-AHEAD, HOP1, HOP2, HOP3, LAG = 0, 1, 2, 3, 4
+HOP1, HOP2, HOP3, LAG = 1, 2, 3, 4
+LATE = ((1, 1),)
 
 
 def kernel(steps, a_ref, b_ref, c_ref, a_buf, b_buf, acc, c_st, snd, rcv, c_snd, c_rcv, c_loc):
@@ -72,7 +74,7 @@
 
     def a_own(ph, q):
         rows, excl, _ = PHASES[ph]
-        carry = pl.ds(al(starts[ph][0] + excl * role_a, 16), rows - excl)
+        carry = pl.ds(al(starts[ph][0] + excl * role_a, 8), rows - excl)
         out = []
         for d, dev in enumerate((dev_yp, dev_ym)):
             for p in range(2):
@@ -83,7 +85,7 @@
 
     def a_fwd(ph, q):
         rows, excl, _ = PHASES[ph]
-        carry = pl.ds(al(starts[ph][0] + excl * role_a, 16), rows - excl)
+        carry = pl.ds(al(starts[ph][0] + excl * role_a, 8), rows - excl)
         out = []
         for d, (blk, dev) in enumerate(((ym, dev_yp), (yp, dev_ym))):
             ref = a_buf.at[q, :, carry, lanes_a(blk, d, SEG)]
@@ -92,7 +94,7 @@
 
     def a_z(ph, q, which):
         rows, excl, _ = PHASES[ph]
-        only = pl.ds(al(starts[ph][0] + (rows - excl) * role_a, 16), excl)
+        only = pl.ds(al(starts[ph][0] + (rows - excl) * role_a, 8), excl)
         ref = a_buf.at[q, :, only, lanes_a((ym, yp, y2)[which])]
         return remote(A_Z, ph, q, ref, ref, dev_za)
 
@@ -205,7 +207,13 @@
         for kind in (A_LOC, B_LOC, A_Z, B_D2D):
             arrived(kind, ph, q)
         for k, (r0, rows, c0, cols) in enumerate(strips(ph)):
-            mm(q, r0, rows, c0, cols)
+            wide = WIDTHS[ph][k]
+
+            def col_tile(j, _, r0=r0, rows=rows, c0=c0, wide=wide):
+                mm(q, r0, rows, al(c0 + j * wide), wide)
+                return 0
+
+            lax.fori_loop(0, cols // wide, col_tile, 0)
 
             @pl.when(q == steps - 1)
             def _(k=k, r0=r0, rows=rows, c0=c0, cols=cols):
@@ -217,8 +225,9 @@
                     return 0
 
                 lax.fori_loop(0, cols // tile, round_tile, 0)
-                for cp in c_copy(ph, k):
-                    cp.start()
+                if (ph, k) not in LATE:
+                    for cp in c_copy(ph, k):
+                        cp.start()
 
     total = len(PHASES) * steps
 
@@ -227,13 +236,18 @@
             q = t - delay - ph * steps
             pl.when(jnp.logical_and(q >= 0, q < steps))(lambda ph=ph, q=q: fn(ph, q))
 
-    for s in range(AHEAD):
-        send_own(s // steps, s % steps)
-
     def body(t, _):
-        stage(t, -AHEAD, send_own)
+        stage(t, 0, send_own)
         stage(t, HOP1, first_hop)
         stage(t, HOP2, second_hop)
+        if LATE:
+
+            @pl.when(t == total - 1 + HOP2)
+            def _():
+                for ph, k in LATE:
+                    for cp in c_copy(ph, k):
+                        cp.start()
+
         stage(t, HOP3, last_hop)
         stage(t, LAG, compute)
         return 0

time: 149 us -> 142 us (0.953); the launches traced: 147 us -> 142 us
  Pallas kernels: 143 us -> 139 us
    pallas_call x1, Pallas kernels: 143 us -> 139 us  [local_mm(): pl.pallas_call(functools.partial(kernel, steps), out_shape=jax.ShapeDtype...]
where the time goes in v3:
time: 142 us
  Pallas kernels  139 us (98%)
  local copies, waits for them, and re-layouts  3.22 us (2%)
    pallas_call x1, Pallas kernels, local_mm(): pl.pallas_call(functools.partial(kernel, steps), out_shape=jax.ShapeDtype...  139 us
    unnamed x1, local copies, waits for them, and re-layouts  3.22 us

profile of v3, /device:TPU:32, one launch (start us, length us, event | category | flops | bytes accessed | tf_op | source)
XLA Modules:
  0.0 141.9 jit_solution(10491046080261146280)
XLA Ops:
  0.0 138.7 %gather_mm.1 = bf16[384,3072]{1,0:T(8,128)(2,1)} custom-call(bf16[4,384,3072]{2,1,0:T(8,128)(2,1)} %bitcast.1, bf16[1536,3072]{1,0:T(8,128)(2,1)} %b_ref.1), custom_call_target="tpu_custom_call" | custom-call | flops 28991029248 | bytes 18874368 | tf_op jit(solution)/shard_map/gather_mm/pallas_call | solution.py:279
  138.7 3.2 %copy.4 = bf16[384,3072]{1,0:T(8,128)(2,1)} copy(bf16[384,3072]{1,0:T(8,128)(2,1)} %gather_mm.1) | data formatting | bytes 4718592

commit v4 on v3

--- a/solution.py
+++ b/solution.py
@@ -192,16 +192,15 @@
         r0, rows, c0, cols = strips(ph)[k]
         dst = c_ref.at[pl.ds(r0, rows), pl.ds(al(col_base + c0), cols)]
         part = (pl.ds(r0, rows), pl.ds(c0, cols))
-        idx = 2 * ph + k
         out = pltpu.make_async_remote_copy(
             src_ref=c_st.at[(1 - e, *part)],
             dst_ref=dst,
-            send_sem=c_snd.at[idx],
-            recv_sem=c_rcv.at[idx],
+            send_sem=c_snd,
+            recv_sem=c_rcv,
             device_id=dev_za,
             device_id_type=MESH,
         )
-        return out, pltpu.make_async_copy(c_st.at[(e, *part)], dst, c_loc.at[idx])
+        return out, pltpu.make_async_copy(c_st.at[(e, *part)], dst, c_loc)
 
     def compute(ph, q):
         for kind in (A_LOC, B_LOC, A_Z, B_D2D):
@@ -263,10 +262,12 @@
     for kind, count in sent_b.items():
         ref = b_buf.at[:, pl.ds(0, count), :]
         pltpu.make_async_copy(ref, ref, snd.at[kind]).wait()
-    for ph in range(len(PHASES)):
-        for k in range(len(strips(ph))):
-            for cp in c_copy(ph, k):
-                cp.wait()
+    for sem in (c_snd, c_rcv, c_loc):
+        pltpu.make_async_copy(c_st.at[0], c_st.at[0], sem).wait()
+
+
+def put_out(c_ref, out_ref):
+    out_ref[...] = c_ref[...]
 
 
 def solution(mesh):
@@ -276,7 +277,7 @@
         band, kblk = a_blk.shape
         sub, half_n, steps = band // 4, kblk // 2, band // SEG
         assert sum(p[0] for p in PHASES) == sub and sum(p[2] for p in PHASES) == half_n
-        return pl.pallas_call(
+        c_blk = pl.pallas_call(
             functools.partial(kernel, steps),
             out_shape=jax.ShapeDtypeStruct((sub, kblk), jnp.bfloat16),
             in_specs=[pl.BlockSpec(memory_space=pl.ANY)] * 2,
@@ -288,9 +289,9 @@
                 pltpu.VMEM((2, sub, half_n), jnp.bfloat16),
                 pltpu.SemaphoreType.DMA((B_Z2,)),
                 pltpu.SemaphoreType.DMA((KINDS, SLOTS)),
-                pltpu.SemaphoreType.DMA((2 * len(PHASES),)),
-                pltpu.SemaphoreType.DMA((2 * len(PHASES),)),
-                pltpu.SemaphoreType.DMA((2 * len(PHASES),)),
+                pltpu.SemaphoreType.DMA,
+                pltpu.SemaphoreType.DMA,
+                pltpu.SemaphoreType.DMA,
             ],
             compiler_params=pltpu.CompilerParams(collective_id=0, has_side_effects=True, vmem_limit_bytes=67043328),
             cost_estimate=pl.CostEstimate(
@@ -298,6 +299,10 @@
             ),
             name="gather_mm",
         )(a_blk.reshape(4, sub, kblk), b_blk)
+        block = pl.BlockSpec((sub // 2, kblk), lambda r: (r, 0))
+        return pl.pallas_call(
+            put_out, grid=(2,), out_shape=jax.ShapeDtypeStruct(c_blk.shape, c_blk.dtype), in_specs=[block], out_specs=block
+        )(c_blk)
 
     spec_in = P("row", "col")
     spec_out = P(("row", "depth"), "col")

time: 142 us -> 141 us (level)
  local copies, waits for them, and re-layouts: 3.22 us -> 0 us
  Pallas kernels: 139 us -> 141 us
    unnamed x1 -> x0, local copies, waits for them, and re-layouts: 3.22 us -> none
    pallas_call x0 -> x1, Pallas kernels: none -> 2.76 us  [local_mm(): pl.pallas_call(put_out, grid=(2,), out_shape=jax.ShapeDtypeStruct(c_blk.s...]
where the time goes in v4:
time: 141 us
  Pallas kernels  141 us (100%)
    pallas_call x1, Pallas kernels, local_mm(): pl.pallas_call(functools.partial(kernel, steps), out_shape=jax.ShapeDtype...  139 us

profile of v4, /device:TPU:32, one launch (start us, length us, event | category | flops | bytes accessed | tf_op | source)
XLA Modules:
  0.0 141.3 jit_solution(16679947350713519019)
XLA Ops:
  0.0 138.6 %gather_mm.1.c_ref = bf16[384,3072]{1,0:T(8,128)(2,1)} custom-call(bf16[4,384,3072]{2,1,0:T(8,128)(2,1)} %bitcast.1, bf16[1536,3072]{1,0:T(8,128)(2,1)} %b_ref.1), custom_call_target="tpu_custom_call" | custom-call | flops 28991029248 | bytes 18874368 | tf_op jit(solution)/shard_map/gather_mm/pallas_call | solution.py:280
  138.6 2.8 %shard_map.28 = bf16[384,3072]{1,0:T(8,128)(2,1)} custom-call(bf16[384,3072]{1,0:T(8,128)(2,1)} %gather_mm.1.c_ref), custom_call_target="tpu_custom_call" | custom-call | tf_op jit(solution)/shard_map/pallas_call | solution.py:303
